TPU v7x, 256 devices: a whole 4x4x8 slice. The times are simulated.
256 devices in a mesh: dp: 16 (over x_hi, z), tensor: 16 (over y, x_lo, core).
Axes of the slice: x: 4 (x_hi: 2, x_lo: 2; x = x_hi * 2 + x_lo), y: 4, z: 8, core: 2. Of those that a mesh axis runs over, the one named last changes fastest.
Arguments:
- tokens: bfloat16 [32768, 4608], P(('dp', 'tensor')), parts along dimension 0, may hold values from -6 to 6
- pre_gain: float32 [4608], replicated, may hold values from 0.1 to 1.9
- query_weight: bfloat16 [4608, 4096], P(None, 'tensor'), as said below
- key_weight: bfloat16 [4608, 2048], P(None, 'tensor'), as said below
- value_weight: bfloat16 [4608, 2048], P(None, 'tensor'), may hold values from -0.09375 to 0.09375
- out_weight: bfloat16 [4096, 4608], P('tensor'), may hold values from -0.09375 to 0.09375
- post_gain: float32 [4608], replicated, may hold values from 0.1 to 1.9
Outputs:
- layer_out: bfloat16 [32768, 4608], P(('dp', 'tensor')), parts along dimension 0
There are 16 independent parts, one for each index of `dp`. A program takes and returns all parts, laid end to end along the dimension named above; an argument that names none is the same for every part. Nothing has to cross between parts.
Inputs may be any that keep to these rules, and one draw needn't show every extreme that they name: `query_weight`: entries lie within 16 / sqrt(4608) of zero. `key_weight`: entries lie within 16 / sqrt(4608) of zero.
All inputs are finite; a program needn't handle non-finite values.
Results may differ from a plain program's by a relative error of at most 0.015.
Values may be sent and summed in bfloat16 or wider, within the bound.
No kernel may reach another device: no remote copies, remote signals or barrier semaphores. Data moves between devices by JAX's collectives and lax.ppermute only.
A program may use at most 192 MiB of HBM per device.

v0:
```python
import jax
import jax.numpy as jnp
from jax import lax
from jax.sharding import PartitionSpec as P

HEAD_DIM = 128
SEQ_LEN = 128
norm_epsilon = 1e-06
soft_cap = 50.0
query_scale = 1.0 / 12.0
rope_base = 10000.0


def rms_scale(vectors, scale_gain):
    mean_square = jnp.mean(vectors * vectors, axis=-1, keepdims=True)
    return vectors * lax.rsqrt(mean_square + norm_epsilon) * scale_gain


def rotate(vectors, positions):
    half_dim = vectors.shape[-1] // 2
    exponent = jnp.arange(half_dim, dtype=jnp.float32) / half_dim
    angles = positions.astype(jnp.float32)[:, None] * jnp.power(rope_base, -exponent)[None, :]
    cosine = jnp.cos(angles)[:, None, :]
    sine_part = jnp.sin(angles)[:, None, :]
    first_half = vectors[..., :half_dim]
    second_half = vectors[..., half_dim:]
    return jnp.concatenate(
        [
            first_half * cosine - second_half * sine_part,
            second_half * cosine + first_half * sine_part,
        ],
        axis=-1,
    )


def project_block(normed, query_weight, key_weight, value_weight):
    block_rows = normed.shape[0]
    positions = jnp.arange(block_rows, dtype=jnp.int32) % SEQ_LEN
    query = jnp.dot(normed, query_weight, preferred_element_type=jnp.float32)
    keys = jnp.dot(normed, key_weight, preferred_element_type=jnp.float32)
    values = jnp.dot(normed, value_weight, preferred_element_type=jnp.float32)
    query = rotate(query.reshape(block_rows, -1, HEAD_DIM), positions).reshape(block_rows, -1)
    keys = rotate(keys.reshape(block_rows, -1, HEAD_DIM), positions).reshape(block_rows, -1)
    return jnp.concatenate(
        [query.astype(jnp.bfloat16), keys.astype(jnp.bfloat16), values.astype(jnp.bfloat16)], axis=1
    )


def attend(query, keys, values, query_pos, key_pos):
    query_count = query.shape[0]
    key_count = keys.shape[0]
    key_heads = keys.shape[1] // HEAD_DIM
    groups = query.shape[1] // keys.shape[1]
    query_four = query.reshape(query_count, key_heads, groups, HEAD_DIM)
    key_three = keys.reshape(key_count, key_heads, HEAD_DIM)
    value_three = values.reshape(key_count, key_heads, HEAD_DIM)
    raw_scores = jnp.einsum(
        "qhgd,khd->hgqk", query_four, key_three, preferred_element_type=jnp.float32
    )
    capped = soft_cap * jnp.tanh(raw_scores * query_scale / soft_cap)
    allowed = jnp.logical_and(
        key_pos[None, :] <= query_pos[:, None],
        key_pos[None, :] // SEQ_LEN == query_pos[:, None] // SEQ_LEN,
    )
    weights = jnp.where(allowed[None, None], jnp.exp(capped), 0.0)
    probability = (weights / jnp.sum(weights, axis=-1, keepdims=True)).astype(jnp.bfloat16)
    mixed = jnp.einsum(
        "hgqk,khd->qhgd", probability, value_three, preferred_element_type=jnp.float32
    )
    return mixed.astype(jnp.bfloat16).reshape(query_count, -1)


def body(tokens, pre_gain, query_weight, key_weight, value_weight, out_weight, post_gain):
    local_rows = tokens.shape[0]
    query_cols = query_weight.shape[1]
    key_cols = key_weight.shape[1]
    normed = rms_scale(tokens.astype(jnp.float32), pre_gain).astype(jnp.bfloat16)
    stacked = project_block(
        lax.all_gather(normed, "tensor", axis=0, tiled=True), query_weight, key_weight, value_weight
    )
    query = stacked[:, :query_cols]
    keys = stacked[:, query_cols : query_cols + key_cols]
    values = stacked[:, query_cols + key_cols :]
    token_count = stacked.shape[0]
    key_count = min(token_count, lax.axis_size("tensor") * local_rows + SEQ_LEN)
    key_first = jnp.clip(jnp.int32(0) // SEQ_LEN * SEQ_LEN, 0, token_count - key_count)
    query_pos = jnp.arange(lax.axis_size("tensor") * local_rows, dtype=jnp.int32)
    key_pos = key_first + jnp.arange(key_count, dtype=jnp.int32)
    block_out = attend(query, keys, values, query_pos, key_pos)
    mixed = lax.psum_scatter(
        jnp.dot(block_out, out_weight, preferred_element_type=jnp.float32).astype(jnp.bfloat16),
        "tensor",
        scatter_dimension=0,
        tiled=True,
    ).astype(jnp.float32)
    branch = rms_scale(mixed, post_gain)
    return (tokens.astype(jnp.float32) + branch).astype(jnp.bfloat16)


def solution(mesh):
    return jax.shard_map(
        body,
        mesh=mesh,
        in_specs=(
            P(("dp", "tensor"), None),
            P(),
            P(None, "tensor"),
            P(None, "tensor"),
            P(None, "tensor"),
            P("tensor", None),
            P(),
        ),
        out_specs=P(("dp", "tensor"), None),
        check_vma=False,
    )
```

profile of v0, /device:TPU:4, one launch (start us, length us, event | category | flops | bytes accessed | tf_op | source)
XLA Modules:
  0.0 423.9 jit_solution(4512877549720790362)
XLA Ops:
  6.5 0.0 copy-start
  6.5 0.0 all-gather.2.cloned.1.call-start
  6.5 1.7 fusion.9
  8.3 2.6 fusion.11
  10.9 0.0 all-gather.2.cloned.1.call-update
  10.9 0.0 reduce-scatter.2.cloned.1.call-start
  11.0 5.6 %multiply_cosine_fusion = (f32[2048,64]{1,0:T(8,128)}, f32[2048,64]{1,0:T(8,128)}) fusion(f32[64]{0:T(128)S(1)} %negate_power_fusion, f32[2048]{0:T(1024)S(1)} %fusion.36), kind=kLoop, calls=%fused_computation.26 | loop fusion | flops 131072 | bytes 1057024 | tf_op jit(solution)/shard_map/cos | solution.py:23
  16.6 5.4 %fusion.3 = pred[2048,2048]{0,1:T(8,128)(4,1)} fusion(s32[2048]{0:T(1024)S(1)} %add_select_fusion), kind=kLoop, calls=%fused_computation.7 | loop fusion | flops 12582912 | bytes 4202496 | tf_op jit(solution)/shard_map/and | solution.py:61
  22.0 96.0 %all-gather.2.cloned.1.call-done = bf16[2048,4608]{1,0:T(8,128)(2,1)} async-done(((bf16[128,4608]{1,0:T(8,128)(2,1)}), bf16[2048,4608]{1,0:T(8,128)(2,1)}) %all-gather.2.cloned.1.call-update) | async-done | bytes 18874384 | tf_op jit(solution)/shard_map/all_gather | solution.py:79
  118.0 10.4 %convolution_bitcast_fusion = f32[2048,1,128]{0,2,1:T(8,128)S(1)} fusion(bf16[2048,4608]{1,0:T(8,128)(2,1)} %all-gather.2.cloned.1.call-done, bf16[4608,128]{1,0:T(8,128)(2,1)} %param.10), kind=kOutput, calls=%fused_computation.14 | convolution fusion | flops 2415919104 | bytes 21102592 | tf_op jit(solution)/shard_map/dot_general | solution.py:40
  128.4 3.0 fusion.29
  131.4 9.7 %fusion.43 = f32[2048,256]{0,1:T(8,128)S(1)} fusion(bf16[2048,4608]{1,0:T(8,128)(2,1)} %all-gather.2.cloned.1.call-done, bf16[4608,256]{1,0:T(8,128)(2,1)} %param.9), kind=kOutput, calls=%fused_computation.66 | convolution fusion | flops 4831838208 | bytes 23330816 | tf_op jit(solution)/shard_map/dot_general | solution.py:39
  141.1 1.2 fusion.42
  142.3 3.2 copy.16
  145.5 1.9 copy.15
  147.4 0.0 copy-start.2
  147.4 4.8 %subtract_convert_fusion = (bf16[2048,2,64]{2,0,1:T(8,128)(2,1)}, bf16[2048,2,64]{2,0,1:T(8,128)(2,1)}) fusion(f32[2048,2,64]{2,0,1:T(8,128)} %copy.16, f32[2048,2,64]{2,0,1:T(8,128)} %copy.15, f32[2048,64]{1,0:T(8,128)} %get-tuple-element.12, f32[2048,64]{1,0:T(8,128)} %get-tuple-element.11), kind=kLoop, calls=%fused_computation.24 | loop fusion | flops 2097152 | bytes 4194304 | tf_op jit(solution)/shard_map/convert
  152.2 0.0 copy-done.2
  152.2 19.2 %fusion = (f32[2,2048]{1,0:T(2,128)S(1)}, f32[2048,2048,2]{1,0,2:T(8,128)}) fusion(pred[2048,2048]{0,1:T(8,128)(4,1)S(1)} %copy-done.2, bf16[2048,2,64]{2,0,1:T(8,128)(2,1)} %get-tuple-element.6, bf16[2048,2,64]{2,0,1:T(8,128)(2,1)} %get-tuple-element.5, bf16[2048,64]{0,1:T(8,128)(2,1)} %get-tuple-element.10, bf16[2048,64]{0,1:T(8,128)(2,1)} %get-tuple-element.9), kind=kOutput, calls=%fused_computation.2 | convolution fusion | flops 2184179712 | bytes 39337984 | tf_op jit(solution)/shard_map/qhgd,khd->hgqk/dot_general | solution.py:57
  171.4 25.0 %fusion.4 = bf16[128,2,2048]{2,0,1:T(8,128)(2,1)S(1)} fusion(f32[2,2048]{1,0:T(2,128)S(1)} %get-tuple-element.13, f32[2048,2048,2]{1,0,2:T(8,128)} %get-tuple-element.14, pred[2048,2048]{0,1:T(8,128)(4,1)} %fusion.3, bf16[2048,4608]{1,0:T(8,128)(2,1)} %all-gather.2.cloned.1.call-done, bf16[4608,128]{1,0:T(8,128)(2,1)} %param.11), kind=kOutput, calls=%fused_computation.13 | convolution fusion | flops 4606132224 | bytes 58867712 | tf_op jit(solution)/shard_map/hgqk,khd->qhgd/dot_general | solution.py:67
  196.4 0.0 copy-done
  196.4 9.5 %convolution_convert_fusion = bf16[2048,4608]{1,0:T(8,128)(2,1)} fusion(bf16[2048,256]{0,1:T(8,128)(2,1)S(1)} %bitcast.48, bf16[256,4608]{1,0:T(8,128)(2,1)S(1)} %copy-done), kind=kOutput, calls=%fused_computation.3 | convolution fusion | flops 4841275392 | bytes 22282240 | tf_op jit(solution)/shard_map/dot_general | solution.py:91
  205.9 0.0 copy-start.1
  205.9 0.0 reduce-scatter.2.cloned.1.call-update
  205.9 206.8 %reduce-scatter.2.cloned.1.call-done = bf16[128,4608]{1,0:T(8,128)(2,1)} async-done(((bf16[2048,4608]{1,0:T(8,128)(2,1)}), bf16[128,4608]{1,0:T(8,128)(2,1)}) %reduce-scatter.2.cloned.1.call-update) | async-done | bytes 1179664 | tf_op jit(solution)/shard_map/reduce_scatter | solution.py:90
  412.7 1.6 fusion.7
  414.3 0.0 copy-done.1
  414.3 2.8 fusion.12
  (5 shorter events, 0.0 us)
Async XLA Ops:
  6.5 189.9 %copy-start = (bf16[256,4608]{1,0:T(8,128)(2,1)S(1)}, bf16[256,4608]{1,0:T(8,128)(2,1)}, u32[]{:S(2)}) copy-start(bf16[256,4608]{1,0:T(8,128)(2,1)} %param.12) | copy-start | bytes 7077892
  6.5 111.4 %all-gather.2.cloned.1.call-start = ((), (), s32[]{:S(2)}) async-start(), calls=%async_computation.1 | async-start | bytes 20054016 | tf_op jit(solution)/shard_map/all_gather | solution.py:79
  10.9 401.8 %reduce-scatter.2.cloned.1.call-start = ((), (), s32[]{:S(2)}) async-start(), calls=%async_computation.2 | async-start | bytes 20054016 | tf_op jit(solution)/shard_map/reduce_scatter | solution.py:90
  147.4 4.8 %copy-start.2 = (pred[2048,2048]{0,1:T(8,128)(4,1)S(1)}, pred[2048,2048]{0,1:T(8,128)(4,1)}, u32[]{:S(2)}) copy-start(pred[2048,2048]{0,1:T(8,128)(4,1)} %fusion.3) | copy-start | bytes 12582916
  205.9 208.4 %copy-start.1 = (bf16[128,4608]{1,0:T(8,128)(2,1)S(1)}, bf16[128,4608]{1,0:T(8,128)(2,1)}, u32[]{:S(2)}) copy-start(bf16[128,4608]{1,0:T(8,128)(2,1)} %param.7) | copy-start | bytes 3538948
Sparse Core Ops, SparseCore 0:
  11.1 106.8 all-gather.1
  206.1 206.6 reduce-scatter.1
where the time goes:
time: 424 us
  waiting for transfers between devices  303 us (71%)
  matrix products  73.8 us (17%)
  other arithmetic  27.6 us (7%)
  between operations  13.5 us (3%)
  local copies, waits for them, and re-layouts  6.26 us (1%)
    reduce_scatter x1, waiting for transfers between devices, body(): lax.psum_scatter(jnp.dot(block_out, out_weight, preferred_element_type=jn...  207 us
    all_gather x1, waiting for transfers between devices, body(): lax.all_gather(normed, 'tensor', axis=0, tiled=True)  96 us
    dot_general x1, matrix products, attend(): jnp.einsum('hgqk,khd->qhgd', probability, value_three, preferred_element_...  25 us
    dot_general x1, matrix products, attend(): jnp.einsum('qhgd,khd->hgqk', query_four, key_three, preferred_element_typ...  19.2 us
    dot_general x1, matrix products, project_block(): keys = jnp.dot(normed, key_weight, preferred_element_type=jnp.float32)  10.4 us
    dot_general x1, matrix products, project_block(): query = jnp.dot(normed, query_weight, preferred_element_type=jnp.float32)  9.69 us
    dot_general x1, matrix products, body(): jnp.dot(block_out, out_weight, preferred_element_type=jnp.float32)  9.5 us
  transfers between devices with their start and end apart: 2, of which 2 were waited for; matrix products, arithmetic and copies ran while one was open for 3% of the time, Pallas kernels for 0%

commit v1 on v0

--- a/solution.py
+++ b/solution.py
@@ -75,9 +75,16 @@
     query_cols = query_weight.shape[1]
     key_cols = key_weight.shape[1]
     normed = rms_scale(tokens.astype(jnp.float32), pre_gain).astype(jnp.bfloat16)
-    stacked = project_block(
-        lax.all_gather(normed, "tensor", axis=0, tiled=True), query_weight, key_weight, value_weight
+    _press_levels_all = lambda work_x: jnp.concatenate(
+        lax.all_to_all(
+            jnp.stack([work_x for _ in range(lax.psum(1, axis_name="tensor"))]),
+            axis_name="tensor",
+            concat_axis=0,
+            split_axis=0,
+        ),
+        axis=0,
     )
+    stacked = project_block(_press_levels_all(normed), query_weight, key_weight, value_weight)
     query = stacked[:, :query_cols]
     keys = stacked[:, query_cols : query_cols + key_cols]
     values = stacked[:, query_cols + key_cols :]

time: 424 us -> 527 us (1.24)
  waiting for transfers between devices: 303 us -> 402 us
  other arithmetic: 27.6 us -> 20.3 us
  local copies, waits for them, and re-layouts: 6.26 us -> 12.2 us
    all_to_all x0 -> x1, waiting for transfers between devices: none -> 195 us  [body(): lax.all_to_all(jnp.stack([work_x for _ in range(lax.psum(1, axis_name='te...]
    all_gather x1 -> x0, waiting for transfers between devices: 96 us -> none  [body(): lax.all_gather(normed, 'tensor', axis=0, tiled=True)]
    another operation x0 -> x1, local copies, waits for them, and re-layouts: none -> 6.67 us  [body(): jnp.stack([work_x for _ in range(lax.psum(1, axis_name='tensor'))])]
  transfers between devices with their start and end apart: 2 -> 2, of which waited for: 2 -> 2; matrix products, arithmetic and copies ran while one was open for 3% -> 2% of each run, Pallas kernels for 0% -> 0%
where the time goes in v1:
time: 527 us
  waiting for transfers between devices  402 us (76%)
  matrix products  73.4 us (14%)
  other arithmetic  20.3 us (4%)
  between operations  13.5 us (3%)
  local copies, waits for them, and re-layouts  12.2 us (2%)
  starting transfers between devices  5.31 us (1%)
    reduce_scatter x1, waiting for transfers between devices, body(): lax.psum_scatter(jnp.dot(block_out, out_weight, preferred_element_type=jn...  207 us
    all_to_all x1, waiting for transfers between devices, body(): lax.all_to_all(jnp.stack([work_x for _ in range(lax.psum(1, axis_name='te...  195 us
    dot_general x1, matrix products, attend(): jnp.einsum('hgqk,khd->qhgd', probability, value_three, preferred_element_...  25 us
    dot_general x1, matrix products, attend(): jnp.einsum('qhgd,khd->hgqk', query_four, key_three, preferred_element_typ...  18.8 us
  transfers between devices with their start and end apart: 2, of which 2 were waited for; matrix products, arithmetic and copies ran while one was open for 2% of the time, Pallas kernels for 0%

profile of v1, /device:TPU:4, one launch (start us, length us, event | category | flops | bytes accessed | tf_op | source)
XLA Modules:
  0.0 526.9 jit_solution(14870005220287142098)
XLA Ops:
  6.5 0.0 copy-start
  6.5 1.7 fusion.9
  8.3 1.6 fusion.11
  9.9 6.7 %stack.2 = bf16[16,128,4608]{2,1,0:T(8,128)(2,1)} broadcast(bf16[128,4608]{1,0:T(8,128)(2,1)S(1)} %fusion.11), dimensions={1,2} | broadcast | bytes 20054016 | tf_op jit(solution)/shard_map/stack | solution.py:80
  16.6 5.3 all-to-all-start
  21.8 0.0 reduce-scatter.2.cloned.1.call-start
  21.9 4.3 copy.16
  26.2 2.8 multiply_cosine_fusion
  29.0 5.4 %fusion.3 = pred[2048,2048]{0,1:T(8,128)(4,1)} fusion(s32[2048]{0:T(1024)S(1)} %add_select_fusion), kind=kLoop, calls=%fused_computation.7 | loop fusion | flops 12582912 | bytes 4202496 | tf_op jit(solution)/shard_map/and | solution.py:61
  34.4 195.1 %all-to-all-done = bf16[16,128,4608]{2,1,0:T(8,128)(2,1)} async-done(((bf16[16,128,4608]{2,1,0:T(8,128)(2,1)}), bf16[16,128,4608]{2,1,0:T(8,128)(2,1)}, u32[]{:S(2)}, u32[]{:S(2)}) %all-to-all-start) | async-done | bytes 18874400 | tf_op jit(solution)/shard_map/all_to_all | solution.py:79
  229.5 10.4 %convolution_bitcast_fusion = f32[2048,1,128]{0,2,1:T(8,128)S(1)} fusion(bf16[2048,4608]{1,0:T(8,128)(2,1)} %bitcast, bf16[4608,128]{1,0:T(8,128)(2,1)} %param.10), kind=kOutput, calls=%fused_computation.14 | convolution fusion | flops 2415919104 | bytes 21102592 | tf_op jit(solution)/shard_map/dot_general | solution.py:40
  239.9 3.0 fusion.29
  242.9 0.0 copy-start.3
  242.9 0.0 copy-start.4
  242.9 9.8 %fusion.42 = f32[2048,2,128]{0,2,1:T(8,128)S(1)} fusion(bf16[2048,4608,1]{1,0,2:T(8,128)(2,1)} %bitcast.6, bf16[2,128,4608]{2,1,0:T(8,128)(2,1)} %bitcast.52), kind=kOutput, calls=%fused_computation.65 | convolution fusion | flops 4831838208 | bytes 23330816 | tf_op jit(solution)/shard_map/dot_general | solution.py:39
  252.7 0.0 copy-start.2
  252.7 0.0 copy-done.3
  252.7 0.0 copy-done.4
  252.7 1.4 subtract_convert_fusion
  254.1 1.2 copy-done.2
  255.3 18.8 %fusion = (f32[2,2048]{1,0:T(2,128)S(1)}, f32[2048,2048,2]{1,0,2:T(8,128)}) fusion(pred[2048,2048]{0,1:T(8,128)(4,1)S(1)} %copy-done.2, bf16[2048,2,64]{0,2,1:T(8,128)(2,1)} %get-tuple-element.6, bf16[2048,2,64]{0,2,1:T(8,128)(2,1)} %get-tuple-element.5, bf16[2048,64]{0,1:T(8,128)(2,1)} %get-tuple-element.8, bf16[2048,64]{0,1:T(8,128)(2,1)} %get-tuple-element.7), kind=kOutput, calls=%fused_computation.2 | convolution fusion | flops 2184179712 | bytes 39337984 | tf_op jit(solution)/shard_map/qhgd,khd->hgqk/dot_general | solution.py:57
  274.1 25.0 %fusion.4 = bf16[128,2,2048]{2,0,1:T(8,128)(2,1)S(1)} fusion(f32[2,2048]{1,0:T(2,128)S(1)} %get-tuple-element.11, f32[2048,2048,2]{1,0,2:T(8,128)} %get-tuple-element.12, pred[2048,2048]{0,1:T(8,128)(4,1)} %fusion.3, bf16[2048,4608]{1,0:T(8,128)(2,1)} %bitcast, bf16[4608,128]{1,0:T(8,128)(2,1)} %param.11), kind=kOutput, calls=%fused_computation.13 | convolution fusion | flops 4606132224 | bytes 58867712 | tf_op jit(solution)/shard_map/hgqk,khd->qhgd/dot_general | solution.py:67
  299.1 0.0 copy-done
  299.1 9.5 %convolution_convert_fusion = bf16[2048,4608]{1,0:T(8,128)(2,1)} fusion(bf16[2048,256]{0,1:T(8,128)(2,1)S(1)} %bitcast.53, bf16[256,4608]{1,0:T(8,128)(2,1)S(1)} %copy-done), kind=kOutput, calls=%fused_computation.3 | convolution fusion | flops 4841275392 | bytes 22282240 | tf_op jit(solution)/shard_map/dot_general | solution.py:98
  308.6 0.0 copy-start.1
  308.6 0.0 reduce-scatter.2.cloned.1.call-update
  308.6 207.1 %reduce-scatter.2.cloned.1.call-done = bf16[128,4608]{1,0:T(8,128)(2,1)} async-done(((bf16[2048,4608]{1,0:T(8,128)(2,1)}), bf16[128,4608]{1,0:T(8,128)(2,1)}) %reduce-scatter.2.cloned.1.call-update) | async-done | bytes 1179664 | tf_op jit(solution)/shard_map/reduce_scatter | solution.py:97
  515.7 1.6 fusion.7
  517.3 0.0 copy-done.1
  517.3 2.8 fusion.12
  (5 shorter events, 0.0 us)
Async XLA Ops:
  6.5 292.5 %copy-start = (bf16[256,4608]{1,0:T(8,128)(2,1)S(1)}, bf16[256,4608]{1,0:T(8,128)(2,1)}, u32[]{:S(2)}) copy-start(bf16[256,4608]{1,0:T(8,128)(2,1)} %param.12) | copy-start | bytes 7077892
  16.6 212.9 %all-to-all-start = ((bf16[16,128,4608]{2,1,0:T(8,128)(2,1)}), bf16[16,128,4608]{2,1,0:T(8,128)(2,1)}, u32[]{:S(2)}, u32[]{:S(2)}) async-start(bf16[16,128,4608]{2,1,0:T(8,128)(2,1)} %stack.2), calls=%async_computation | async-start | bytes 37748736 | tf_op jit(solution)/shard_map/all_to_all | solution.py:79
  21.8 493.8 %reduce-scatter.2.cloned.1.call-start = ((), (), s32[]{:S(2)}) async-start(), calls=%async_computation.2 | async-start | bytes 20054016 | tf_op jit(solution)/shard_map/reduce_scatter | solution.py:97
  242.9 9.8 %copy-start.3 = (f32[2048,64]{0,1:T(8,128)S(1)}, f32[2048,64]{0,1:T(8,128)}, u32[]{:S(2)}) copy-start(f32[2048,64]{0,1:T(8,128)} %get-tuple-element.9) | copy-start | bytes 1572868
  242.9 9.8 %copy-start.4 = (f32[2048,64]{0,1:T(8,128)S(1)}, f32[2048,64]{0,1:T(8,128)}, u32[]{:S(2)}) copy-start(f32[2048,64]{0,1:T(8,128)} %get-tuple-element.10) | copy-start | bytes 1572868
  252.7 2.6 copy-start.2
  308.6 208.7 %copy-start.1 = (bf16[128,4608]{1,0:T(8,128)(2,1)S(1)}, bf16[128,4608]{1,0:T(8,128)(2,1)}, u32[]{:S(2)}) copy-start(bf16[128,4608]{1,0:T(8,128)(2,1)} %param.7) | copy-start | bytes 3538948
Sparse Core Ops, SparseCore 0:
  308.7 206.9 reduce-scatter.1
